TPU v7x, 32 devices: a whole 2x2x4 slice. The times are simulated.
32 devices in a mesh: grp: 8 (over y, x, core), blk: 4 (over z).
Axes of the slice: x: 2, y: 2, z: 4, core: 2. Of those that a mesh axis runs over, the one named last changes fastest.
Arguments:
- visual: bfloat16 [24576, 3584], P(('grp', 'blk')), may hold values from -6 to 6
- text_queries: float32 [1024, 3584], P(('grp', 'blk')), may hold values from -100 to 100
- kv_weight: bfloat16 [3584, 1024], replicated, may hold values from -0.09375 to 0.09375
- placement: int32 [3072, 1], P(('grp', 'blk')), may hold values from 0 to 31; in each aligned block of 96 rows (0 to 95, 96 to 191, ...) at most 4 rows name the same one
Outputs:
- attended: float32 [1024, 3584], P(('grp', 'blk'))
Inputs may be any that keep to these rules, and one draw needn't show every extreme that they name: `placement`: among the 96 blocks of one frame owner at most 4 name the same attention owner, a bound that some block reaches; every attention owner is named by some block.
All inputs are finite; a program needn't handle non-finite values.
Results may differ from a plain program's by a relative error of at most 0.0003.
Values sent between devices are 32-bit elements; how exact they have to be, the bound alone decides.
A program may use at most 128 MiB of HBM per device.

v0:
```python
import functools

import jax
import jax.numpy as jnp
from jax import lax
from jax.experimental import pallas as pl
from jax.experimental.pallas import tpu as pltpu
from jax.sharding import PartitionSpec as P

HEADS = 28
KV_HEADS = 4
MESH = pl.DeviceIdType.MESH
F32 = jnp.float32
BF16 = jnp.bfloat16
NT = (((1,), (1,)), ((), ()))


def dot(a, b):
    return jnp.dot(a, b, preferred_element_type=F32)


def split3(x):
    hi = x.astype(BF16)
    rest = x - hi.astype(F32)
    mid = rest.astype(BF16)
    low = (rest - mid.astype(F32)).astype(BF16)
    return hi, mid, low


def kernel(
    n_grp, n_blk, per_seg, group, dim,
    visual_hbm, query_hbm, weight_hbm, place_ref,
    out_ref,
    visual, weight, pieces, outgoing, arrived, queries,
    counts_out, counts_in, bias, kcat_a, kcat_b, v_t, p_hi, p_lo,
    stats_out, stats_in, partial, partial_in,
    load_sem, weight_sem, query_load_sem,
    query_send, query_recv, count_send, count_recv,
    kv_send, kv_recv, stat_send, stat_recv, part_send, part_recv,
):
    me_g = lax.axis_index("grp")
    me_b = lax.axis_index("blk")
    rows = query_hbm.shape[0]
    n_rows = visual.shape[0]
    blocks = place_ref.shape[0]
    block_rows = n_rows // blocks
    seg_rows = per_seg * block_rows
    lanes = n_blk * rows
    kv_heads = KV_HEADS
    scale = dim ** (-0.5)

    query_load = pltpu.make_async_copy(query_hbm, queries.at[me_b], query_load_sem)
    query_load.start()
    visual_load = pltpu.make_async_copy(visual_hbm, visual, load_sem)
    visual_load.start()

    def weight_loads(h):
        slot = h % 2
        return [
            pltpu.make_async_copy(
                weight_hbm.at[:, pl.ds((half * kv_heads + h) * dim, dim)],
                weight.at[slot, :, pl.ds(half * dim, dim)],
                weight_sem.at[slot, half],
            )
            for half in range(2)
        ]

    for h in range(2):
        for copy in weight_loads(h):
            copy.start()

    barrier = pltpu.get_barrier_semaphore()
    for d in range(1, n_grp):
        pl.semaphore_signal(
            barrier, inc=1, device_id={"grp": lax.rem(me_g + d, n_grp)}, device_id_type=MESH
        )
    for e in range(1, n_blk):
        pl.semaphore_signal(
            barrier, inc=1, device_id={"blk": lax.rem(me_b + e, n_blk)}, device_id_type=MESH
        )
    pl.semaphore_wait(barrier, n_grp + n_blk - 2)

    query_load.wait()
    query_copies = []
    for e in range(1, n_blk):
        copy = pltpu.make_async_remote_copy(
            src_ref=queries.at[me_b],
            dst_ref=queries.at[me_b],
            send_sem=query_send.at[e],
            recv_sem=query_recv.at[e],
            device_id={"blk": lax.rem(me_b + e, n_blk)},
            device_id_type=MESH,
        )
        copy.start()
        query_copies.append(copy)

    owner = place_ref[...]
    seg = jnp.zeros_like(owner)
    for g in range(1, n_grp):
        seg += (owner >= g * n_blk).astype(jnp.int32)
    block_id = lax.broadcasted_iota(jnp.int32, (blocks, n_rows), 0)
    row_id = lax.broadcasted_iota(jnp.int32, (blocks, n_rows), 1)
    first = block_id * block_rows
    within = (row_id >= first) & (row_id < first + block_rows)
    before = row_id >= first + block_rows
    seg_wide = jnp.broadcast_to(seg, (blocks, n_rows))
    row_seg = jnp.sum(jnp.where(within, seg_wide, 0), axis=0, keepdims=True)
    row_in = jnp.sum(jnp.where(within, row_id - first, 0), axis=0, keepdims=True)
    rank = jnp.sum(
        jnp.where(before & (seg_wide == row_seg), 1, 0), axis=0, keepdims=True
    )
    row_slot = row_seg * seg_rows + rank * block_rows + row_in

    for g in range(n_grp):
        count = jnp.sum((seg == g).astype(F32), axis=0, keepdims=True) * block_rows
        counts_out[g] = jnp.broadcast_to(count, counts_out.shape[1:])

    kv_copies = []
    count_copies = []
    visual_load.wait()
    tile = min(256, n_rows)
    for h in range(kv_heads):
        for copy in weight_loads(h):
            copy.wait()

        def project(i, _, slot=h % 2):
            at = pl.ds(pl.multiple_of(i * tile, tile), tile)
            hi, mid, low = split3(dot(visual[at, :], weight[slot]))
            pieces[at, 0 : 2 * dim] = hi
            pieces[at, 2 * dim : 4 * dim] = mid
            pieces[at, 4 * dim : 6 * dim] = low
            return 0

        lax.fori_loop(0, n_rows // tile, project, 0)
        if h + 2 < kv_heads:
            for copy in weight_loads(h + 2):
                copy.start()

        def pack(g, _, h=h):
            slot_id = lax.broadcasted_iota(jnp.int32, (seg_rows, n_rows), 0) + g * seg_rows
            pick = jnp.where(slot_id == row_slot, 1.0, 0.0).astype(BF16)
            both = dot(pick, pieces[...])
            both = both[:, : 2 * dim] + both[:, 2 * dim : 4 * dim] + both[:, 4 * dim :]
            outgoing[2 * h, g] = both[:, :dim]
            outgoing[2 * h + 1, g] = both[:, dim:]
            return 0

        lax.fori_loop(0, n_grp, pack, 0)
        for half in range(2):
            unit = 2 * h + half
            row = []
            for d in range(1, n_grp):
                peer = lax.rem(me_g + d, n_grp)
                copy = pltpu.make_async_remote_copy(
                    src_ref=outgoing.at[unit, peer],
                    dst_ref=arrived.at[unit, d],
                    send_sem=kv_send.at[unit, d],
                    recv_sem=kv_recv.at[unit, d],
                    device_id={"grp": peer},
                    device_id_type=MESH,
                )
                copy.start()
                row.append(copy)
            kv_copies.append(row)
            arrived[unit, 0] = outgoing[unit, me_g]
        if h == 0:
            for d in range(1, n_grp):
                peer = lax.rem(me_g + d, n_grp)
                copy = pltpu.make_async_remote_copy(
                    src_ref=counts_out.at[peer],
                    dst_ref=counts_in.at[d],
                    send_sem=count_send.at[d],
                    recv_sem=count_recv.at[d],
                    device_id={"grp": peer},
                    device_id_type=MESH,
                )
                copy.start()
                count_copies.append(copy)
            counts_in[0] = counts_out[me_g]

    for copy in query_copies:
        copy.wait_recv()
    for copy in count_copies:
        copy.wait_recv()
    key_id = lax.broadcasted_iota(jnp.int32, (seg_rows, 128), 0).astype(F32)
    for d in range(n_grp):
        bias[d * seg_rows : (d + 1) * seg_rows, :] = jnp.where(
            key_id < counts_in[d][0:1, :], 0.0, -1e30
        )

    keys = n_grp * seg_rows
    stat_copies = []
    part_copies = []
    for h in range(kv_heads):
        for copy in kv_copies[2 * h]:
            copy.wait_recv()
        hi, mid, low = split3(arrived[2 * h].reshape(keys, dim))
        kcat_a[:, :dim] = hi
        kcat_a[:, dim:] = mid
        kcat_b[:, :dim] = hi
        kcat_b[:, dim:] = low

        stats_out[h] = jnp.zeros_like(stats_out[h])

        def score(j, _, h=h):
            at = pl.ds(pl.multiple_of((h * group + j) * dim, dim), dim)
            q = queries[:, :, at].reshape(lanes, dim)
            hi, mid, low = split3(q)
            s = lax.dot_general(
                kcat_a[...], jnp.concatenate([hi, hi], 1), NT, preferred_element_type=F32
            )
            t = lax.dot_general(
                kcat_a[...], jnp.concatenate([mid, mid], 1), NT, preferred_element_type=F32
            )
            u = lax.dot_general(
                kcat_b[...], jnp.concatenate([low, hi], 1), NT, preferred_element_type=F32
            )
            b = bias[...]
            if lanes > 128:
                b = jnp.concatenate([b] * (lanes // 128), 1)
            s = (s + (t + u)) * scale + b
            peak = jnp.max(s, axis=0, keepdims=True)
            p = jnp.exp(s - peak)
            total = jnp.sum(p, axis=0, keepdims=True)
            hi = p.astype(BF16)
            p_hi[j] = hi
            p_lo[j] = (p - hi.astype(F32)).astype(BF16)
            stats_out[h, 0, pl.ds(j, 1), :] = peak
            stats_out[h, 1, pl.ds(j, 1), :] = total
            return 0

        lax.fori_loop(0, group, score, 0)
        row = []
        for e in range(1, n_blk):
            copy = pltpu.make_async_remote_copy(
                src_ref=stats_out.at[h],
                dst_ref=stats_in.at[h, e],
                send_sem=stat_send.at[h, e],
                recv_sem=stat_recv.at[h, e],
                device_id={"blk": lax.rem(me_b + e, n_blk)},
                device_id_type=MESH,
            )
            copy.start()
            row.append(copy)
        stat_copies.append(row)

        for copy in kv_copies[2 * h + 1]:
            copy.wait_recv()
        v = arrived[2 * h + 1].reshape(keys, dim).T
        hi = v.astype(BF16)
        v_t[:dim, :] = hi
        v_t[dim:, :] = (v - hi.astype(F32)).astype(BF16)
        for copy in row:
            copy.wait_recv()
        mine = stats_out[h, 0]
        top = mine
        for e in range(1, n_blk):
            top = jnp.maximum(top, stats_in[h, e, 0])
        factor = jnp.exp(mine - top)
        whole = stats_out[h, 1] * factor
        for e in range(1, n_blk):
            whole += stats_in[h, e, 1] * jnp.exp(stats_in[h, e, 0] - top)
        stats_in[h, 0, 0] = factor / whole

        def mix(j, _, h=h):
            o = dot(v_t[...], p_hi[j])
            o = o[:dim] + o[dim:] + dot(v_t[:dim, :], p_lo[j])
            o = (o * stats_in[h, 0, 0, pl.ds(j, 1), :]).T
            at = pl.ds(pl.multiple_of(j * dim, dim), dim)
            partial[h, :, :, at] = o.reshape(n_blk, rows, dim)
            return 0

        lax.fori_loop(0, group, mix, 0)
        row = []
        for e in range(1, n_blk):
            peer = lax.rem(me_b + e, n_blk)
            copy = pltpu.make_async_remote_copy(
                src_ref=partial.at[h, peer],
                dst_ref=partial_in.at[h, e - 1],
                send_sem=part_send.at[h, e],
                recv_sem=part_recv.at[h, e],
                device_id={"blk": peer},
                device_id_type=MESH,
            )
            copy.start()
            row.append(copy)
        part_copies.append(row)

    for h in range(kv_heads):
        for copy in part_copies[h]:
            copy.wait_recv()
        total = partial[h, me_b]
        for e in range(1, n_blk):
            total += partial_in[h, e - 1]
        out_ref[:, h * group * dim : (h + 1) * group * dim] = total

    for row in [query_copies, count_copies] + kv_copies + stat_copies + part_copies:
        for copy in row:
            copy.wait_send()


def on_device(n_grp, n_blk, visual, text_queries, kv_weight, placement):
    n_rows, model = visual.shape
    rows, wide = text_queries.shape
    dim = kv_weight.shape[1] // (2 * KV_HEADS)
    group = wide // dim // KV_HEADS
    blocks = placement.shape[0]
    block_rows = n_rows // blocks
    per_pair = max(2, blocks // (n_grp * n_blk) + 1)
    per_seg = n_blk * per_pair
    seg_rows = per_seg * block_rows
    keys = n_grp * seg_rows
    lanes = n_blk * rows
    heads = KV_HEADS
    units = 2 * heads
    stat_rows = -(-group // 8) * 8
    any_space = pl.BlockSpec(memory_space=pl.ANY)
    in_vmem = pl.BlockSpec(memory_space=pltpu.VMEM)
    dma = pltpu.SemaphoreType.DMA
    return pl.pallas_call(
        functools.partial(kernel, n_grp, n_blk, per_seg, group, dim),
        name="routed_attention",
        out_shape=jax.ShapeDtypeStruct((rows, wide), F32),
        in_specs=[any_space, any_space, any_space, in_vmem],
        out_specs=in_vmem,
        scratch_shapes=[
            pltpu.VMEM((n_rows, model), BF16),
            pltpu.VMEM((2, model, 2 * dim), BF16),
            pltpu.VMEM((n_rows, 6 * dim), BF16),
            pltpu.VMEM((units, n_grp, seg_rows, dim), F32),
            pltpu.VMEM((units, n_grp, seg_rows, dim), F32),
            pltpu.VMEM((n_blk, rows, wide), F32),
            pltpu.VMEM((n_grp, 8, 128), F32),
            pltpu.VMEM((n_grp, 8, 128), F32),
            pltpu.VMEM((keys, 128), F32),
            pltpu.VMEM((keys, 2 * dim), BF16),
            pltpu.VMEM((keys, 2 * dim), BF16),
            pltpu.VMEM((2 * dim, keys), BF16),
            pltpu.VMEM((group, keys, lanes), BF16),
            pltpu.VMEM((group, keys, lanes), BF16),
            pltpu.VMEM((heads, 2, stat_rows, lanes), F32),
            pltpu.VMEM((heads, n_blk, 2, stat_rows, lanes), F32),
            pltpu.VMEM((heads, n_blk, rows, group * dim), F32),
            pltpu.VMEM((heads, n_blk - 1, rows, group * dim), F32),
            dma,
            dma((2, 2)),
            dma,
            dma((n_blk,)),
            dma((n_blk,)),
            dma((n_grp,)),
            dma((n_grp,)),
            dma((units, n_grp)),
            dma((units, n_grp)),
            dma((heads, n_blk)),
            dma((heads, n_blk)),
            dma((heads, n_blk)),
            dma((heads, n_blk)),
        ],
        compiler_params=pltpu.CompilerParams(
            collective_id=0, has_side_effects=True, vmem_limit_bytes=67043328
        ),
    )(visual, text_queries, kv_weight, placement)


def solution(mesh):
    placed = (P(("grp", "blk"), None), P(("grp", "blk"), None), P(), P(("grp", "blk"), None))
    body = functools.partial(on_device, mesh.shape["grp"], mesh.shape["blk"])
    return jax.shard_map(
        body, mesh=mesh, in_specs=placed, out_specs=P(("grp", "blk"), None), check_vma=False
    )
```

profile of v0, /device:TPU:0, one launch (start us, length us, event | category | flops | bytes accessed | tf_op | source)
XLA Modules:
  0.0 117.2 jit_solution(5235197841756488498)
XLA Ops:
  0.0 1.4 %copy.5.place_ref = s32[96,1]{1,0:T(8,128)} copy(s32[96,1]{0,1:T(1,128)} %param.7) | data formatting | bytes 768 | tf_op args[3]
  1.4 114.0 %routed_attention.1 = f32[32,3584]{1,0:T(8,128)} custom-call(bf16[768,3584]{1,0:T(8,128)(2,1)} %visual_hbm.1, f32[32,3584]{1,0:T(8,128)} %query_hbm.1, bf16[3584,1024]{1,0:T(8,128)(2,1)} %weight_hbm.1, s32[96,1]{1,0:T(8,128)} %copy.5.place_ref), custom_call_target="tpu_custom_call" | custom-call | tf_op jit(solution)/shard_map/routed_attention/pallas_call | solution.py:320
  115.4 1.8 %copy.7 = f32[32,3584]{1,0:T(8,128)} copy(f32[32,3584]{1,0:T(8,128)} %routed_attention.1) | data formatting | bytes 917504
where the time goes:
time: 117 us
  Pallas kernels  114 us (97%)
  local copies, waits for them, and re-layouts  3.19 us (3%)
    pallas_call x1, Pallas kernels, on_device(): pl.pallas_call(functools.partial(kernel, n_grp, n_blk, per_seg, group, di...  114 us
    unnamed x2, local copies, waits for them, and re-layouts  3.19 us

commit v1 on v0

v1 whole, which is shorter than its diff:
```python
import functools
import math

import jax
import jax.numpy as jnp
from jax import lax
from jax.experimental import pallas as pl
from jax.experimental.pallas import tpu as pltpu
from jax.sharding import PartitionSpec as P

HEADS = 28
KV_HEADS = 4
MESH = pl.DeviceIdType.MESH
F32 = jnp.float32
BF16 = jnp.bfloat16
NT = (((1,), (1,)), ((), ()))


def dot(a, b):
    return jnp.dot(a, b, preferred_element_type=F32)


def split2(x):
    hi = x.astype(BF16)
    return hi, (x - hi.astype(F32)).astype(BF16)


def kernel(
    n_grp, n_blk, per_seg, group, dim,
    visual_hbm, query_hbm, weight_hbm, place_ref,
    out_ref,
    visual, weight, kv, outgoing, arrived, queries, index_v, index_s,
    counts_out, counts_in, bias, kcat, v_t, scores, probs,
    stats_out, stats_in, partial, partial_in,
    load_sem, weight_sem, query_load_sem, index_sem,
    query_send, query_recv, count_send, count_recv,
    kv_send, kv_recv, stat_send, stat_recv, part_send, part_recv,
):
    me_g = lax.axis_index("grp")
    me_b = lax.axis_index("blk")
    rows = query_hbm.shape[0]
    n_rows = visual.shape[0]
    blocks = place_ref.shape[0]
    block_rows = n_rows // blocks
    seg_rows = per_seg * block_rows
    lanes = n_blk * rows
    keys = n_grp * seg_rows
    slots = n_grp * per_seg
    heads = KV_HEADS
    wide = group * dim
    scale = dim ** (-0.5) * math.log2(math.e)
    tile = load_rows(n_rows)
    tiles = n_rows // tile

    def weight_loads(h):
        return [
            pltpu.make_async_copy(
                weight_hbm.at[:, pl.ds((half * heads + h) * dim, dim)],
                weight.at[h % 2, :, pl.ds(half * dim, dim)],
                weight_sem.at[h % 2, half],
            )
            for half in range(2)
        ]

    def visual_load(i):
        at = pl.ds(pl.multiple_of(i * tile, tile), tile)
        return pltpu.make_async_copy(visual_hbm.at[at, :], visual.at[at, :], load_sem.at[i])

    query_load = pltpu.make_async_copy(query_hbm, queries.at[me_b], query_load_sem)
    for copy in weight_loads(0):
        copy.start()
    visual_load(0).start()
    query_load.start()
    for i in range(1, tiles):
        visual_load(i).start()

    barrier = pltpu.get_barrier_semaphore()
    for d in range(1, n_grp):
        pl.semaphore_signal(
            barrier, inc=1, device_id={"grp": lax.rem(me_g + d, n_grp)}, device_id_type=MESH
        )
    for e in range(1, n_blk):
        pl.semaphore_signal(
            barrier, inc=1, device_id={"blk": lax.rem(me_b + e, n_blk)}, device_id_type=MESH
        )

    owner = place_ref[...]
    seg = jnp.zeros_like(owner)
    for g in range(1, n_grp):
        seg += (owner >= g * n_blk).astype(jnp.int32)
    block_id = lax.broadcasted_iota(jnp.int32, (blocks, slots), 0)
    slot_id = lax.broadcasted_iota(jnp.int32, (blocks, slots), 1)
    slot_seg = jnp.zeros_like(slot_id)
    for g in range(1, n_grp):
        slot_seg += (slot_id >= g * per_seg).astype(jnp.int32)
    inside = jnp.broadcast_to(seg, (blocks, slots)) == slot_seg
    member = inside.astype(jnp.int32)
    running = member
    shift = 1
    while shift < blocks:
        running += jnp.where(block_id >= shift, pltpu.roll(running, shift, 0), 0)
        shift *= 2
    hit = inside & (running - member == slot_id - slot_seg * per_seg)
    index = jnp.sum(jnp.where(hit, block_id, 0), axis=0, keepdims=True)
    index_v[...] = jnp.broadcast_to(index, index_v.shape)
    index_copy = pltpu.make_async_copy(index_v, index_s, index_sem)
    index_copy.start()
    for d in range(n_grp):
        g = lax.rem(me_g + d, n_grp)
        count = jnp.sum((seg == g).astype(F32), axis=0, keepdims=True) * block_rows
        counts_out[d] = jnp.broadcast_to(count, counts_out.shape[1:])
    counts_in[0] = counts_out[0]

    pl.semaphore_wait(barrier, n_grp + n_blk - 2)

    def query_path(way, hop):
        step = 1 if way == 0 else n_blk - 1
        source = lax.rem(me_b + hop * (n_blk - step), n_blk)
        peer = lax.rem(me_b + step, n_blk)
        if way == 0:
            ok = jnp.logical_and(me_b >= hop, me_b < n_blk - 1)
        else:
            ok = jnp.logical_and(me_b < n_blk - hop, me_b >= 1)
        return source, peer, ok

    def query_copy(way, hop, h):
        source, peer, ok = query_path(way, hop)
        cols = pl.ds(h * wide, wide)
        copy = pltpu.make_async_remote_copy(
            src_ref=queries.at[source, :, cols],
            dst_ref=queries.at[source, :, cols],
            send_sem=query_send.at[way, hop, h],
            recv_sem=query_recv.at[way, hop + 1, h],
            device_id={"blk": peer},
            device_id_type=MESH,
        )
        return copy, ok

    def query_arrival(way, hop, h):
        source = query_path(way, hop)[0]
        at = queries.at[source, :, pl.ds(h * wide, wide)]
        return pltpu.make_async_copy(at, at, query_recv.at[way, hop, h])

    def query_send_on(hop, h):
        for way in range(2):
            copy, ok = query_copy(way, hop, h)

            @pl.when(ok)
            def _(copy=copy, way=way):
                if hop > 0:
                    query_arrival(way, hop, h).wait()
                copy.start()

    def query_wait(h):
        for way in range(2):
            for hop in range(1, n_blk):
                @pl.when(me_b == (n_blk - 1 if way == 0 else 0))
                def _(copy=query_arrival(way, hop, h)):
                    copy.wait()

    relay_points = {}
    first_point = [0, 2, 4, 5]
    for h in range(heads):
        limit = 3 if h == 0 else 3 + 2 * h
        for hop in range(1, n_blk - 1):
            point = min(first_point[min(h, 3)] + (hop - 1) * (2 if h == 0 else 1), limit)
            relay_points.setdefault(point, []).append((hop, h))
    relay_points.setdefault(1, []).append((0, 2))
    relay_points.setdefault(3, []).append((0, 3))

    def relay(point):
        for hop, h in sorted(relay_points.get(point, []), key=lambda t: (t[1], t[0])):
            query_send_on(hop, h)

    def kv_copy(unit, d):
        return pltpu.make_async_remote_copy(
            src_ref=outgoing.at[unit, d - 1],
            dst_ref=arrived.at[unit, d],
            send_sem=kv_send.at[unit, d],
            recv_sem=kv_recv.at[unit, d],
            device_id={"grp": lax.rem(me_g + d, n_grp)},
            device_id_type=MESH,
        )

    def count_copy(d):
        return pltpu.make_async_remote_copy(
            src_ref=counts_out.at[d],
            dst_ref=counts_in.at[d],
            send_sem=count_send.at[d],
            recv_sem=count_recv.at[d],
            device_id={"grp": lax.rem(me_g + d, n_grp)},
            device_id_type=MESH,
        )

    query_load.wait()
    query_send_on(0, 0)
    query_send_on(0, 1)

    for h in range(heads):
        for copy in weight_loads(h):
            copy.wait()

        def project(i, _, h=h):
            if h == 0:
                visual_load(i).wait()
            at = pl.ds(pl.multiple_of(i * tile, tile), tile)
            to = pl.ds(i * (tile // block_rows), tile // block_rows)
            kv[to] = dot(visual[at, :], weight[h % 2]).reshape(-1, block_rows, 2 * dim)
            return 0

        if h == 0:
            for copy in weight_loads(1):
                copy.start()
        lax.fori_loop(0, tiles, project, 0)
        if h + 2 < heads:
            for copy in weight_loads(h + 2):
                copy.start()
        if h == 0:
            index_copy.wait()

        def pack(d, target, place, h=h):
            first = lax.rem(me_g + d, n_grp) * per_seg
            for r in range(per_seg):
                block = index_s[0, first + r]
                both = kv[block]
                to = pl.ds(r * block_rows, block_rows)
                target[2 * h, place, to, :] = both[:, :dim]
                target[2 * h + 1, place, to, :] = both[:, dim:]

        def pack_peer(d, _):
            pack(d, outgoing, d - 1)
            return 0

        lax.fori_loop(1, n_grp, pack_peer, 0)
        for unit in (2 * h, 2 * h + 1):
            for d in range(1, n_grp):
                kv_copy(unit, d).start()
        pack(0, arrived, 0)
        if h == 0:
            for d in range(1, n_grp):
                count_copy(d).start()
        relay(h)

    for d in range(1, n_grp):
        count_copy(d).wait_recv()
    key_id = lax.broadcasted_iota(jnp.int32, (seg_rows, 128), 0).astype(F32)
    for d in range(n_grp):
        bias[d * seg_rows : (d + 1) * seg_rows, :] = jnp.where(
            key_id < counts_in[d][0:1, :], 0.0, -1e30
        )

    def stat_copy(h, e):
        return pltpu.make_async_remote_copy(
            src_ref=stats_out.at[h],
            dst_ref=stats_in.at[h, e],
            send_sem=stat_send.at[h, e],
            recv_sem=stat_recv.at[h, e],
            device_id={"blk": lax.rem(me_b + e, n_blk)},
            device_id_type=MESH,
        )

    def part_copy(h, e):
        peer = lax.rem(me_b + e, n_blk)
        return pltpu.make_async_remote_copy(
            src_ref=partial.at[h, peer],
            dst_ref=partial_in.at[h, e - 1],
            send_sem=part_send.at[h, e],
            recv_sem=part_recv.at[h, e],
            device_id={"blk": peer},
            device_id_type=MESH,
        )

    for h in range(heads):
        query_wait(h)
        for d in range(1, n_grp):
            kv_copy(2 * h, d).wait_recv()
        hi, low = split2(arrived[2 * h].reshape(keys, dim))
        kcat[:, :dim] = hi
        kcat[:, dim:] = low
        stats_out[h] = jnp.zeros_like(stats_out[h])

        def score(j, slot, h=h):
            at = pl.ds(pl.multiple_of((h * group + j) * dim, dim), dim)
            hi, low = split2(queries[:, :, at].reshape(lanes, dim) * scale)
            both = jnp.concatenate(
                [jnp.concatenate([hi, hi], 1), jnp.concatenate([low, low], 1)], 0
            )
            s = lax.dot_general(kcat[...], both, NT, preferred_element_type=F32)
            b = bias[...]
            if lanes > 128:
                b = jnp.concatenate([b] * (lanes // 128), 1)
            s = s[:, :lanes] + s[:, lanes:] + b
            scores[slot] = s
            stats_out[h, 0, pl.ds(j, 1), :] = jnp.max(s, axis=0, keepdims=True)

        def weigh(j, slot, h=h):
            p = jnp.exp2(scores[slot] - stats_out[h, 0, pl.ds(j, 1), :])
            stats_out[h, 1, pl.ds(j, 1), :] = jnp.sum(p, axis=0, keepdims=True)
            hi, low = split2(p)
            probs[j, :, :lanes] = hi
            probs[j, :, lanes:] = low

        score(0, 0)

        def step(i, _):
            score(2 * i + 1, 1)
            weigh(2 * i, 0)
            score(2 * i + 2, 0)
            weigh(2 * i + 1, 1)
            return 0

        pairs = (group - 1) // 2
        lax.fori_loop(0, pairs, step, 0)
        if group % 2 == 0:
            score(group - 1, 1)
        weigh(2 * pairs, 0)
        if group % 2 == 0:
            weigh(group - 1, 1)
        for e in range(1, n_blk):
            stat_copy(h, e).start()
        relay(4 + 2 * h)

        for d in range(1, n_grp):
            kv_copy(2 * h + 1, d).wait_recv()
        hi, low = split2(arrived[2 * h + 1].reshape(keys, dim).T)
        v_t[:dim, :] = hi
        v_t[dim:, :] = low
        for e in range(1, n_blk):
            stat_copy(h, e).wait_recv()
        mine = stats_out[h, 0]
        top = mine
        for e in range(1, n_blk):
            top = jnp.maximum(top, stats_in[h, e, 0])
        factor = jnp.exp2(mine - top)
        whole = stats_out[h, 1] * factor
        for e in range(1, n_blk):
            whole += stats_in[h, e, 1] * jnp.exp2(stats_in[h, e, 0] - top)
        stats_in[h, 0, 0] = factor / whole

        def mix(j, _, h=h):
            o = dot(v_t[...], probs[j])
            o = (o[:dim, :lanes] + o[dim:, :lanes]) + (o[:dim, lanes:] + o[dim:, lanes:])
            o = (o * stats_in[h, 0, 0, pl.ds(j, 1), :]).T
            at = pl.ds(pl.multiple_of(j * dim, dim), dim)
            partial[h, :, :, at] = o.reshape(n_blk, rows, dim)
            return 0

        lax.fori_loop(0, group, mix, 0)
        for e in range(1, n_blk):
            part_copy(h, e).start()
        relay(5 + 2 * h)

    for h in range(heads):
        for e in range(1, n_blk):
            part_copy(h, e).wait_recv()
        total = partial[h, me_b]
        for e in range(1, n_blk):
            total += partial_in[h, e - 1]
        out_ref[:, h * wide : (h + 1) * wide] = total

    for h in range(heads):
        for hop in range(n_blk - 1):
            for way in range(2):
                copy, ok = query_copy(way, hop, h)

                @pl.when(ok)
                def _(copy=copy):
                    copy.wait_send()
        for d in range(1, n_grp):
            kv_copy(2 * h, d).wait_send()
            kv_copy(2 * h + 1, d).wait_send()
        for e in range(1, n_blk):
            stat_copy(h, e).wait_send()
            part_copy(h, e).wait_send()
    for d in range(1, n_grp):
        count_copy(d).wait_send()


def load_rows(n_rows):
    return math.gcd(256, n_rows)


def on_device(n_grp, n_blk, visual, text_queries, kv_weight, placement):
    n_rows, model = visual.shape
    rows, wide = text_queries.shape
    dim = kv_weight.shape[1] // (2 * KV_HEADS)
    group = wide // dim // KV_HEADS
    blocks = placement.shape[0]
    block_rows = n_rows // blocks
    per_pair = max(2, blocks // (n_grp * n_blk) + 1)
    per_seg = n_blk * per_pair
    seg_rows = per_seg * block_rows
    keys = n_grp * seg_rows
    slots = n_grp * per_seg
    lanes = n_blk * rows
    heads = KV_HEADS
    units = 2 * heads
    stat_rows = -(-group // 8) * 8
    tiles = n_rows // load_rows(n_rows)
    any_space = pl.BlockSpec(memory_space=pl.ANY)
    in_vmem = pl.BlockSpec(memory_space=pltpu.VMEM)
    dma = pltpu.SemaphoreType.DMA
    return pl.pallas_call(
        functools.partial(kernel, n_grp, n_blk, per_seg, group, dim),
        name="routed_attention",
        out_shape=jax.ShapeDtypeStruct((rows, wide), F32),
        in_specs=[any_space, any_space, any_space, in_vmem],
        out_specs=in_vmem,
        scratch_shapes=[
            pltpu.VMEM((n_rows, model), BF16),
            pltpu.VMEM((2, model, 2 * dim), BF16),
            pltpu.VMEM((blocks, block_rows, 2 * dim), F32),
            pltpu.VMEM((units, n_grp - 1, seg_rows, dim), F32),
            pltpu.VMEM((units, n_grp, seg_rows, dim), F32),
            pltpu.VMEM((n_blk, rows, wide), F32),
            pltpu.VMEM((8, slots), jnp.int32),
            pltpu.SMEM((8, slots), jnp.int32),
            pltpu.VMEM((n_grp, 8, 128), F32),
            pltpu.VMEM((n_grp, 8, 128), F32),
            pltpu.VMEM((keys, 128), F32),
            pltpu.VMEM((keys, 2 * dim), BF16),
            pltpu.VMEM((2 * dim, keys), BF16),
            pltpu.VMEM((2, keys, lanes), F32),
            pltpu.VMEM((group, keys, 2 * lanes), BF16),
            pltpu.VMEM((heads, 2, stat_rows, lanes), F32),
            pltpu.VMEM((heads, n_blk, 2, stat_rows, lanes), F32),
            pltpu.VMEM((heads, n_blk, rows, group * dim), F32),
            pltpu.VMEM((heads, n_blk - 1, rows, group * dim), F32),
            dma((tiles,)),
            dma((2, 2)),
            dma,
            dma,
            dma((2, n_blk, heads)),
            dma((2, n_blk, heads)),
            dma((n_grp,)),
            dma((n_grp,)),
            dma((units, n_grp)),
            dma((units, n_grp)),
            dma((heads, n_blk)),
            dma((heads, n_blk)),
            dma((heads, n_blk)),
            dma((heads, n_blk)),
        ],
        compiler_params=pltpu.CompilerParams(
            collective_id=0, has_side_effects=True, vmem_limit_bytes=67043328
        ),
    )(visual, text_queries, kv_weight, placement)


def solution(mesh):
    placed = (P(("grp", "blk"), None), P(("grp", "blk"), None), P(), P(("grp", "blk"), None))
    body = functools.partial(on_device, mesh.shape["grp"], mesh.shape["blk"])
    return jax.shard_map(
        body, mesh=mesh, in_specs=placed, out_specs=P(("grp", "blk"), None), check_vma=False
    )
```

time: 117 us -> 93.9 us (0.80)
  Pallas kernels: 114 us -> 90.5 us
    pallas_call x1, Pallas kernels: 114 us -> 90.5 us  [on_device(): pl.pallas_call(functools.partial(kernel, n_grp, n_blk, per_seg, group, di...]
where the time goes in v1:
time: 93.9 us; the launch traced here: 93.7 us
  Pallas kernels  90.5 us (96%)
  local copies, waits for them, and re-layouts  3.19 us (3%)
    pallas_call x1, Pallas kernels, on_device(): pl.pallas_call(functools.partial(kernel, n_grp, n_blk, per_seg, group, di...  90.5 us
    unnamed x2, local copies, waits for them, and re-layouts  3.19 us

profile of v1, /device:TPU:0, one launch (start us, length us, event | category | flops | bytes accessed | tf_op | source)
XLA Modules:
  0.0 93.7 jit_solution(9962374739333483767)
XLA Ops:
  0.0 1.4 %copy.5.place_ref = s32[96,1]{1,0:T(8,128)} copy(s32[96,1]{0,1:T(1,128)} %param.7) | data formatting | bytes 768 | tf_op args[3]
  1.4 90.5 %routed_attention.1 = f32[32,3584]{1,0:T(8,128)} custom-call(bf16[768,3584]{1,0:T(8,128)(2,1)} %visual_hbm.1, f32[32,3584]{1,0:T(8,128)} %query_hbm.1, bf16[3584,1024]{1,0:T(8,128)(2,1)} %weight_hbm.1, s32[96,1]{1,0:T(8,128)} %copy.5.place_ref), custom_call_target="tpu_custom_call" | custom-call | tf_op jit(solution)/shard_map/routed_attention/pallas_call | solution.py:403
  91.9 1.8 %copy.7 = f32[32,3584]{1,0:T(8,128)} copy(f32[32,3584]{1,0:T(8,128)} %routed_attention.1) | data formatting | bytes 917504

commit v2 on v1

--- a/solution.py
+++ b/solution.py
@@ -31,10 +31,10 @@
     out_ref,
     visual, weight, kv, outgoing, arrived, queries, index_v, index_s,
     counts_out, counts_in, bias, kcat, v_t, scores, probs,
-    stats_out, stats_in, partial, partial_in,
+    stats_out, stats_in, partial, partial_in, summed,
     load_sem, weight_sem, query_load_sem, index_sem,
     query_send, query_recv, count_send, count_recv,
-    kv_send, kv_recv, stat_send, stat_recv, part_send, part_recv,
+    kv_send, kv_recv, stat_send, stat_recv, part_send, part_recv, chain_send, chain_recv,
 ):
     me_g = lax.axis_index("grp")
     me_b = lax.axis_index("blk")
@@ -259,16 +259,71 @@
             device_id_type=MESH,
         )
 
-    def part_copy(h, e):
+    cuts = part_cuts(group)
+    parts = len(cuts) - 1
+
+    def part_copy(part, e):
         peer = lax.rem(me_b + e, n_blk)
+        cols = pl.ds(cuts[part] * dim, (cuts[part + 1] - cuts[part]) * dim)
         return pltpu.make_async_remote_copy(
-            src_ref=partial.at[h, peer],
-            dst_ref=partial_in.at[h, e - 1],
-            send_sem=part_send.at[h, e],
-            recv_sem=part_recv.at[h, e],
+            src_ref=partial.at[heads - 1, peer, :, cols],
+            dst_ref=partial_in.at[e - 1, :, cols],
+            send_sem=part_send.at[part, e],
+            recv_sem=part_recv.at[part, e],
             device_id={"blk": peer},
             device_id_type=MESH,
         )
+
+    def chain_copy(h, way, dest):
+        step = 1 if way == 0 else n_blk - 1
+        return pltpu.make_async_remote_copy(
+            src_ref=partial.at[h, dest],
+            dst_ref=summed.at[h, dest + 1 - way],
+            send_sem=chain_send.at[h, way, dest],
+            recv_sem=chain_recv.at[h, way, dest],
+            device_id={"blk": lax.rem(me_b + step, n_blk)},
+            device_id_type=MESH,
+        )
+
+    def chain_dests(way, stage):
+        far = range(n_blk - 1, stage, -1)
+        return [d if way == 0 else n_blk - 1 - d for d in far]
+
+    def at_stage(way, stage):
+        return pl.when(me_b == (stage if way == 0 else n_blk - 1 - stage))
+
+    def chain(h, stage):
+        for way in range(2):
+            @at_stage(way, stage)
+            def _(way=way):
+                for dest in chain_dests(way, stage):
+                    copy = chain_copy(h, way, dest)
+                    if stage > 0:
+                        copy.wait_recv()
+                        partial[h, dest] += summed[h, dest + 1 - way]
+                    copy.start()
+
+    def chain_end(h):
+        cols = slice(h * wide, (h + 1) * wide)
+        out_ref[:, cols] = partial[h, me_b]
+        for way in range(2):
+            @pl.when(me_b > 0 if way == 0 else me_b < n_blk - 1)
+            def _(way=way):
+                chain_copy(h, way, me_b).wait_recv()
+                out_ref[:, cols] += summed[h, me_b + 1 - way]
+
+    def chains(point):
+        for h in range(heads - 1):
+            if point == 5 + 2 * h:
+                chain(h, 0)
+            elif point == 6 + 2 * h:
+                for stage in range(1, min(2, n_blk - 1)):
+                    chain(h, stage)
+            elif point == 7 + 2 * h:
+                for stage in range(2, n_blk - 1):
+                    chain(h, stage)
+            elif point == 8 + 2 * h:
+                chain_end(h)
 
     for h in range(heads):
         query_wait(h)
@@ -319,6 +374,7 @@
         for e in range(1, n_blk):
             stat_copy(h, e).start()
         relay(4 + 2 * h)
+        chains(4 + 2 * h)
 
         for d in range(1, n_grp):
             kv_copy(2 * h + 1, d).wait_recv()
@@ -337,27 +393,43 @@
             whole += stats_in[h, e, 1] * jnp.exp2(stats_in[h, e, 0] - top)
         stats_in[h, 0, 0] = factor / whole
 
-        def mix(j, _, h=h):
+        def mix(j, h=h):
             o = dot(v_t[...], probs[j])
             o = (o[:dim, :lanes] + o[dim:, :lanes]) + (o[:dim, lanes:] + o[dim:, lanes:])
-            o = (o * stats_in[h, 0, 0, pl.ds(j, 1), :]).T
-            at = pl.ds(pl.multiple_of(j * dim, dim), dim)
-            partial[h, :, :, at] = o.reshape(n_blk, rows, dim)
-            return 0
-
-        lax.fori_loop(0, group, mix, 0)
-        for e in range(1, n_blk):
-            part_copy(h, e).start()
+            o = o * stats_in[h, 0, 0, j : j + 1, :]
+            partial[h, :, :, j * dim : (j + 1) * dim] = o.T.reshape(n_blk, rows, dim)
+
+        for part in range(parts):
+            for j in range(cuts[part], cuts[part + 1]):
+                mix(j)
+            if h == heads - 1:
+                for e in range(1, n_blk):
+                    part_copy(part, e).start()
         relay(5 + 2 * h)
-
-    for h in range(heads):
-        for e in range(1, n_blk):
-            part_copy(h, e).wait_recv()
-        total = partial[h, me_b]
-        for e in range(1, n_blk):
-            total += partial_in[h, e - 1]
-        out_ref[:, h * wide : (h + 1) * wide] = total
-
+        chains(5 + 2 * h)
+
+    for point in range(4 + 2 * heads, 7 + 2 * heads):
+        chains(point)
+    for part in range(parts):
+        for e in range(1, n_blk):
+            part_copy(part, e).wait_recv()
+        cols = slice(cuts[part] * dim, cuts[part + 1] * dim)
+        total = partial[heads - 1, me_b, :, cols]
+        for e in range(1, n_blk):
+            total += partial_in[e - 1, :, cols]
+        first = (heads - 1) * wide
+        out_ref[:, first + cols.start : first + cols.stop] = total
+
+    for h in range(heads - 1):
+        for stage in range(n_blk - 1):
+            for way in range(2):
+                @at_stage(way, stage)
+                def _(way=way):
+                    for dest in chain_dests(way, stage):
+                        chain_copy(h, way, dest).wait_send()
+    for part in range(parts):
+        for e in range(1, n_blk):
+            part_copy(part, e).wait_send()
     for h in range(heads):
         for hop in range(n_blk - 1):
             for way in range(2):
@@ -371,9 +443,12 @@
             kv_copy(2 * h + 1, d).wait_send()
         for e in range(1, n_blk):
             stat_copy(h, e).wait_send()
-            part_copy(h, e).wait_send()
     for d in range(1, n_grp):
         count_copy(d).wait_send()
+
+
+def part_cuts(group):
+    return sorted({0, min(2, group), min(4, group), group})
 
 
 def load_rows(n_rows):
@@ -397,6 +472,7 @@
     units = 2 * heads
     stat_rows = -(-group // 8) * 8
     tiles = n_rows // load_rows(n_rows)
+    parts = len(part_cuts(group)) - 1
     any_space = pl.BlockSpec(memory_space=pl.ANY)
     in_vmem = pl.BlockSpec(memory_space=pltpu.VMEM)
     dma = pltpu.SemaphoreType.DMA
@@ -425,7 +501,8 @@
             pltpu.VMEM((heads, 2, stat_rows, lanes), F32),
             pltpu.VMEM((heads, n_blk, 2, stat_rows, lanes), F32),
             pltpu.VMEM((heads, n_blk, rows, group * dim), F32),
-            pltpu.VMEM((heads, n_blk - 1, rows, group * dim), F32),
+            pltpu.VMEM((n_blk - 1, rows, group * dim), F32),
+            pltpu.VMEM((heads - 1, n_blk + 1, rows, group * dim), F32),
             dma((tiles,)),
             dma((2, 2)),
             dma,
@@ -438,8 +515,10 @@
             dma((units, n_grp)),
             dma((heads, n_blk)),
             dma((heads, n_blk)),
-            dma((heads, n_blk)),
-            dma((heads, n_blk)),
+            dma((parts, n_blk)),
+            dma((parts, n_blk)),
+            dma((heads - 1, 2, n_blk)),
+            dma((heads - 1, 2, n_blk)),
         ],
         compiler_params=pltpu.CompilerParams(
             collective_id=0, has_side_effects=True, vmem_limit_bytes=67043328

time: 93.9 us -> 80.8 us (0.86)
  Pallas kernels: 90.5 us -> 77.3 us
    pallas_call x1, Pallas kernels: 90.5 us -> 77.3 us  [on_device(): pl.pallas_call(functools.partial(kernel, n_grp, n_blk, per_seg, group, di...]
where the time goes in v2:
time: 80.8 us; the launch traced here: 80.5 us
  Pallas kernels  77.3 us (96%)
  local copies, waits for them, and re-layouts  3.19 us (4%)
    pallas_call x1, Pallas kernels, on_device(): pl.pallas_call(functools.partial(kernel, n_grp, n_blk, per_seg, group, di...  77.3 us
    unnamed x2, local copies, waits for them, and re-layouts  3.19 us

profile of v2, /device:TPU:0, one launch (start us, length us, event | category | flops | bytes accessed | tf_op | source)
XLA Modules:
  0.0 80.5 jit_solution(7253705032781231433)
XLA Ops:
  0.0 1.4 %copy.5.place_ref = s32[96,1]{1,0:T(8,128)} copy(s32[96,1]{0,1:T(1,128)} %param.7) | data formatting | bytes 768 | tf_op args[3]
  1.4 77.3 %routed_attention.1 = f32[32,3584]{1,0:T(8,128)} custom-call(bf16[768,3584]{1,0:T(8,128)(2,1)} %visual_hbm.1, f32[32,3584]{1,0:T(8,128)} %query_hbm.1, bf16[3584,1024]{1,0:T(8,128)(2,1)} %weight_hbm.1, s32[96,1]{1,0:T(8,128)} %copy.5.place_ref), custom_call_target="tpu_custom_call" | custom-call | tf_op jit(solution)/shard_map/routed_attention/pallas_call | solution.py:479
  78.7 1.8 %copy.7 = f32[32,3584]{1,0:T(8,128)} copy(f32[32,3584]{1,0:T(8,128)} %routed_attention.1) | data formatting | bytes 917504

commit v3 on v2

--- a/solution.py
+++ b/solution.py
@@ -9,6 +9,7 @@
 from jax.sharding import PartitionSpec as P
 
 HEADS = 28
+CHAINED = 3
 KV_HEADS = 4
 MESH = pl.DeviceIdType.MESH
 F32 = jnp.float32
@@ -27,12 +28,12 @@
 
 def kernel(
     n_grp, n_blk, per_seg, group, dim,
-    visual_hbm, query_hbm, weight_hbm, place_ref,
+    visual_hbm, query_hbm, weight_hbm, place_hbm,
     out_ref,
-    visual, weight, kv, outgoing, arrived, queries, index_v, index_s,
+    place_ref, visual, weight, kv, outgoing, arrived, queries, index_v, index_s,
     counts_out, counts_in, bias, kcat, v_t, scores, probs,
-    stats_out, stats_in, partial, partial_in, summed,
-    load_sem, weight_sem, query_load_sem, index_sem,
+    stats_out, stats_in, mixing, partial, partial_in, summed,
+    load_sem, weight_sem, query_load_sem, place_sem, index_sem,
     query_send, query_recv, count_send, count_recv,
     kv_send, kv_recv, stat_send, stat_recv, part_send, part_recv, chain_send, chain_recv,
 ):
@@ -40,7 +41,7 @@
     me_b = lax.axis_index("blk")
     rows = query_hbm.shape[0]
     n_rows = visual.shape[0]
-    blocks = place_ref.shape[0]
+    blocks = place_ref.shape[1]
     block_rows = n_rows // blocks
     seg_rows = per_seg * block_rows
     lanes = n_blk * rows
@@ -67,6 +68,8 @@
         return pltpu.make_async_copy(visual_hbm.at[at, :], visual.at[at, :], load_sem.at[i])
 
     query_load = pltpu.make_async_copy(query_hbm, queries.at[me_b], query_load_sem)
+    place_load = pltpu.make_async_copy(place_hbm, place_ref, place_sem)
+    place_load.start()
     for copy in weight_loads(0):
         copy.start()
     visual_load(0).start()
@@ -84,7 +87,8 @@
             barrier, inc=1, device_id={"blk": lax.rem(me_b + e, n_blk)}, device_id_type=MESH
         )
 
-    owner = place_ref[...]
+    place_load.wait()
+    owner = jnp.broadcast_to(place_ref[...], (slots, blocks)).T
     seg = jnp.zeros_like(owner)
     for g in range(1, n_grp):
         seg += (owner >= g * n_blk).astype(jnp.int32)
@@ -93,7 +97,7 @@
     slot_seg = jnp.zeros_like(slot_id)
     for g in range(1, n_grp):
         slot_seg += (slot_id >= g * per_seg).astype(jnp.int32)
-    inside = jnp.broadcast_to(seg, (blocks, slots)) == slot_seg
+    inside = seg == slot_seg
     member = inside.astype(jnp.int32)
     running = member
     shift = 1
@@ -107,11 +111,9 @@
     index_copy.start()
     for d in range(n_grp):
         g = lax.rem(me_g + d, n_grp)
-        count = jnp.sum((seg == g).astype(F32), axis=0, keepdims=True) * block_rows
+        count = jnp.sum((seg[:, :128] == g).astype(F32), axis=0, keepdims=True) * block_rows
         counts_out[d] = jnp.broadcast_to(count, counts_out.shape[1:])
     counts_in[0] = counts_out[0]
-
-    pl.semaphore_wait(barrier, n_grp + n_blk - 2)
 
     def query_path(way, hop):
         step = 1 if way == 0 else n_blk - 1
@@ -192,10 +194,6 @@
             device_id_type=MESH,
         )
 
-    query_load.wait()
-    query_send_on(0, 0)
-    query_send_on(0, 1)
-
     for h in range(heads):
         for copy in weight_loads(h):
             copy.wait()
@@ -232,9 +230,15 @@
             return 0
 
         lax.fori_loop(1, n_grp, pack_peer, 0)
+        if h == 0:
+            query_load.wait()
+            pl.semaphore_wait(barrier, n_grp + n_blk - 2)
+            query_send_on(0, 0)
         for unit in (2 * h, 2 * h + 1):
             for d in range(1, n_grp):
                 kv_copy(unit, d).start()
+        if h == 0:
+            query_send_on(0, 1)
         pack(0, arrived, 0)
         if h == 0:
             for d in range(1, n_grp):
@@ -262,17 +266,44 @@
     cuts = part_cuts(group)
     parts = len(cuts) - 1
 
-    def part_copy(part, e):
+    def part_copy(h, part, e):
         peer = lax.rem(me_b + e, n_blk)
         cols = pl.ds(cuts[part] * dim, (cuts[part + 1] - cuts[part]) * dim)
         return pltpu.make_async_remote_copy(
-            src_ref=partial.at[heads - 1, peer, :, cols],
-            dst_ref=partial_in.at[e - 1, :, cols],
-            send_sem=part_send.at[part, e],
-            recv_sem=part_recv.at[part, e],
+            src_ref=partial.at[h, peer, :, cols],
+            dst_ref=partial_in.at[h - CHAINED, e - 1, :, cols],
+            send_sem=part_send.at[h - CHAINED, part, e],
+            recv_sem=part_recv.at[h - CHAINED, part, e],
             device_id={"blk": peer},
             device_id_type=MESH,
         )
+
+    def head_weights(h):
+        for e in range(1, n_blk):
+            stat_copy(h, e).wait_recv()
+        tops = [stats_out[h, 0]] + [stats_in[h, e, 0] for e in range(1, n_blk)]
+        sums = [stats_out[h, 1]] + [stats_in[h, e, 1] for e in range(1, n_blk)]
+        top = functools.reduce(jnp.maximum, tops)
+        factors = [jnp.exp2(t - top) for t in tops]
+        whole = functools.reduce(jnp.add, [s * f for s, f in zip(sums, factors)])
+        if h < CHAINED:
+            stats_in[h, 0, 0] = factors[0] / whole
+        else:
+            mixing[h - CHAINED] = jnp.concatenate([f / whole for f in factors], 0).T
+
+    def combine(h):
+        mine = mixing[h - CHAINED, pl.ds(pl.multiple_of(me_b * rows, rows), rows), :]
+        stat_rows = stats_out.shape[2]
+        for part in range(parts):
+            for e in range(1, n_blk):
+                part_copy(h, part, e).wait_recv()
+            for j in range(cuts[part], cuts[part + 1]):
+                at = slice(j * dim, (j + 1) * dim)
+                total = partial[h, me_b, :, at] * mine[:, j : j + 1]
+                for e in range(1, n_blk):
+                    col = e * stat_rows + j
+                    total += partial_in[h - CHAINED, e - 1, :, at] * mine[:, col : col + 1]
+                out_ref[:, h * wide + j * dim : h * wide + (j + 1) * dim] = total
 
     def chain_copy(h, way, dest):
         step = 1 if way == 0 else n_blk - 1
@@ -313,7 +344,7 @@
                 out_ref[:, cols] += summed[h, me_b + 1 - way]
 
     def chains(point):
-        for h in range(heads - 1):
+        for h in range(CHAINED):
             if point == 5 + 2 * h:
                 chain(h, 0)
             elif point == 6 + 2 * h:
@@ -381,55 +412,44 @@
         hi, low = split2(arrived[2 * h + 1].reshape(keys, dim).T)
         v_t[:dim, :] = hi
         v_t[dim:, :] = low
-        for e in range(1, n_blk):
-            stat_copy(h, e).wait_recv()
-        mine = stats_out[h, 0]
-        top = mine
-        for e in range(1, n_blk):
-            top = jnp.maximum(top, stats_in[h, e, 0])
-        factor = jnp.exp2(mine - top)
-        whole = stats_out[h, 1] * factor
-        for e in range(1, n_blk):
-            whole += stats_in[h, e, 1] * jnp.exp2(stats_in[h, e, 0] - top)
-        stats_in[h, 0, 0] = factor / whole
+        if h < CHAINED:
+            head_weights(h)
 
         def mix(j, h=h):
             o = dot(v_t[...], probs[j])
             o = (o[:dim, :lanes] + o[dim:, :lanes]) + (o[:dim, lanes:] + o[dim:, lanes:])
-            o = o * stats_in[h, 0, 0, j : j + 1, :]
+            if h < CHAINED:
+                o = o * stats_in[h, 0, 0, j : j + 1, :]
             partial[h, :, :, j * dim : (j + 1) * dim] = o.T.reshape(n_blk, rows, dim)
 
         for part in range(parts):
             for j in range(cuts[part], cuts[part + 1]):
                 mix(j)
-            if h == heads - 1:
+            if h >= CHAINED:
                 for e in range(1, n_blk):
-                    part_copy(part, e).start()
+                    part_copy(h, part, e).start()
         relay(5 + 2 * h)
         chains(5 + 2 * h)
+        if h >= CHAINED:
+            head_weights(h)
+        if h > CHAINED:
+            combine(h - 1)
 
     for point in range(4 + 2 * heads, 7 + 2 * heads):
         chains(point)
-    for part in range(parts):
-        for e in range(1, n_blk):
-            part_copy(part, e).wait_recv()
-        cols = slice(cuts[part] * dim, cuts[part + 1] * dim)
-        total = partial[heads - 1, me_b, :, cols]
-        for e in range(1, n_blk):
-            total += partial_in[e - 1, :, cols]
-        first = (heads - 1) * wide
-        out_ref[:, first + cols.start : first + cols.stop] = total
-
-    for h in range(heads - 1):
+    combine(heads - 1)
+
+    for h in range(CHAINED):
         for stage in range(n_blk - 1):
             for way in range(2):
                 @at_stage(way, stage)
                 def _(way=way):
                     for dest in chain_dests(way, stage):
                         chain_copy(h, way, dest).wait_send()
-    for part in range(parts):
-        for e in range(1, n_blk):
-            part_copy(part, e).wait_send()
+    for h in range(CHAINED, heads):
+        for part in range(parts):
+            for e in range(1, n_blk):
+                part_copy(h, part, e).wait_send()
     for h in range(heads):
         for hop in range(n_blk - 1):
             for way in range(2):
@@ -473,6 +493,7 @@
     stat_rows = -(-group // 8) * 8
     tiles = n_rows // load_rows(n_rows)
     parts = len(part_cuts(group)) - 1
+    direct = heads - CHAINED
     any_space = pl.BlockSpec(memory_space=pl.ANY)
     in_vmem = pl.BlockSpec(memory_space=pltpu.VMEM)
     dma = pltpu.SemaphoreType.DMA
@@ -480,9 +501,10 @@
         functools.partial(kernel, n_grp, n_blk, per_seg, group, dim),
         name="routed_attention",
         out_shape=jax.ShapeDtypeStruct((rows, wide), F32),
-        in_specs=[any_space, any_space, any_space, in_vmem],
+        in_specs=[any_space, any_space, any_space, any_space],
         out_specs=in_vmem,
         scratch_shapes=[
+            pltpu.VMEM((1, blocks), jnp.int32),
             pltpu.VMEM((n_rows, model), BF16),
             pltpu.VMEM((2, model, 2 * dim), BF16),
             pltpu.VMEM((blocks, block_rows, 2 * dim), F32),
@@ -500,11 +522,13 @@
             pltpu.VMEM((group, keys, 2 * lanes), BF16),
             pltpu.VMEM((heads, 2, stat_rows, lanes), F32),
             pltpu.VMEM((heads, n_blk, 2, stat_rows, lanes), F32),
+            pltpu.VMEM((direct, lanes, n_blk * stat_rows), F32),
             pltpu.VMEM((heads, n_blk, rows, group * dim), F32),
-            pltpu.VMEM((n_blk - 1, rows, group * dim), F32),
-            pltpu.VMEM((heads - 1, n_blk + 1, rows, group * dim), F32),
+            pltpu.VMEM((direct, n_blk - 1, rows, group * dim), F32),
+            pltpu.VMEM((CHAINED, n_blk + 1, rows, group * dim), F32),
             dma((tiles,)),
             dma((2, 2)),
+            dma,
             dma,
             dma,
             dma((2, n_blk, heads)),
@@ -515,15 +539,15 @@
             dma((units, n_grp)),
             dma((heads, n_blk)),
             dma((heads, n_blk)),
-            dma((parts, n_blk)),
-            dma((parts, n_blk)),
-            dma((heads - 1, 2, n_blk)),
-            dma((heads - 1, 2, n_blk)),
+            dma((direct, parts, n_blk)),
+            dma((direct, parts, n_blk)),
+            dma((CHAINED, 2, n_blk)),
+            dma((CHAINED, 2, n_blk)),
         ],
         compiler_params=pltpu.CompilerParams(
             collective_id=0, has_side_effects=True, vmem_limit_bytes=67043328
         ),
-    )(visual, text_queries, kv_weight, placement)
+    )(visual, text_queries, kv_weight, placement.reshape(1, blocks))
 
 
 def solution(mesh):

time: 80.8 us -> 76.6 us (0.948)
  Pallas kernels: 77.3 us -> 74.6 us
  local copies, waits for them, and re-layouts: 3.19 us -> 1.82 us
    pallas_call x1, Pallas kernels: 77.3 us -> 74.6 us  [on_device(): pl.pallas_call(functools.partial(kernel, n_grp, n_blk, per_seg, group, di...]
    unnamed x2 -> x1, local copies, waits for them, and re-layouts: 3.19 us -> 1.82 us
where the time goes in v3:
time: 76.6 us; the launch traced here: 76.5 us
  Pallas kernels  74.6 us (97%)
  local copies, waits for them, and re-layouts  1.82 us (2%)
    pallas_call x1, Pallas kernels, on_device(): pl.pallas_call(functools.partial(kernel, n_grp, n_blk, per_seg, group, di...  74.6 us
    unnamed x1, local copies, waits for them, and re-layouts  1.82 us

profile of v3, /device:TPU:0, one launch (start us, length us, event | category | flops | bytes accessed | tf_op | source)
XLA Modules:
  0.0 76.5 jit_solution(12124619994271862952)
XLA Ops:
  0.0 74.6 %routed_attention.1 = f32[32,3584]{1,0:T(8,128)} custom-call(bf16[768,3584]{1,0:T(8,128)(2,1)} %visual_hbm.1, f32[32,3584]{1,0:T(8,128)} %query_hbm.1, bf16[3584,1024]{1,0:T(8,128)(2,1)} %weight_hbm.1, s32[1,96]{1,0:T(1,128)} %bitcast.1), custom_call_target="tpu_custom_call" | custom-call | tf_op jit(solution)/shard_map/routed_attention/pallas_call | solution.py:500
  74.6 1.8 %copy.6 = f32[32,3584]{1,0:T(8,128)} copy(f32[32,3584]{1,0:T(8,128)} %routed_attention.1) | data formatting | bytes 917504

commit v4 on v3

--- a/solution.py
+++ b/solution.py
@@ -468,7 +468,7 @@
 
 
 def part_cuts(group):
-    return sorted({0, min(2, group), min(4, group), group})
+    return sorted({0, min(3, group), group})
 
 
 def load_rows(n_rows):

time: 76.6 us -> 76.4 us (level)
  no operation moved by 1% of the time
where the time goes in v4:
time: 76.4 us; the launch traced here: 76.2 us
  Pallas kernels  74.4 us (97%)
  local copies, waits for them, and re-layouts  1.82 us (2%)
    pallas_call x1, Pallas kernels, on_device(): pl.pallas_call(functools.partial(kernel, n_grp, n_blk, per_seg, group, di...  74.4 us
    unnamed x1, local copies, waits for them, and re-layouts  1.82 us

profile of v4, /device:TPU:0, one launch (start us, length us, event | category | flops | bytes accessed | tf_op | source)
XLA Modules:
  0.0 76.2 jit_solution(4131614706930217794)
XLA Ops:
  0.0 74.4 %routed_attention.1 = f32[32,3584]{1,0:T(8,128)} custom-call(bf16[768,3584]{1,0:T(8,128)(2,1)} %visual_hbm.1, f32[32,3584]{1,0:T(8,128)} %query_hbm.1, bf16[3584,1024]{1,0:T(8,128)(2,1)} %weight_hbm.1, s32[1,96]{1,0:T(1,128)} %bitcast.1), custom_call_target="tpu_custom_call" | custom-call | tf_op jit(solution)/shard_map/routed_attention/pallas_call | solution.py:500
  74.4 1.8 %copy.6 = f32[32,3584]{1,0:T(8,128)} copy(f32[32,3584]{1,0:T(8,128)} %routed_attention.1) | data formatting | bytes 917504
